TPU v7x, 32 devices: a whole 2x2x4 slice. The times are simulated.
32 devices in a mesh: ctx: 16 (over z, x, core), fsdp: 2 (over y).
Axes of the slice: x: 2, y: 2, z: 4, core: 2. Of those that a mesh axis runs over, the one named last changes fastest.
Arguments:
- tokens: bfloat16 [2, 2048, 1024], P('fsdp', 'ctx'), may hold values from -6 to 6
- cotangent: bfloat16 [2, 2048, 1024], P('fsdp', 'ctx'), may hold values from -6 to 6
- gain_attn: float32 [1024], replicated, may hold values from 0.5 to 1.5
- gain_mlp: float32 [1024], replicated, may hold values from 0.5 to 1.5
- qkv_weight: bfloat16 [3072, 1024], P('fsdp'), may hold values from -2 to 2
- out_weight: bfloat16 [1024, 1024], P('fsdp'), may hold values from -0.625 to 0.625
- in_weight: bfloat16 [5248, 1024], P('fsdp'), may hold values from -0.1875 to 0.1875
- down_weight: bfloat16 [1024, 2624], P('fsdp'), may hold values from -0.125 to 0.125
Outputs:
- output: float32 [2, 2048, 1024], P('fsdp', 'ctx')
- grad_input: float32 [2, 2048, 1024], P('fsdp', 'ctx')
- grad_qkv: float32 [3072, 1024], P(('ctx', 'fsdp'))
- grad_out_proj: float32 [1024, 1024], P(('ctx', 'fsdp'))
- grad_in_proj: float32 [5248, 1024], P(('ctx', 'fsdp'))
- grad_down: float32 [1024, 2624], P(('ctx', 'fsdp'))
- grad_gain_attn: float32 [1024], P(('ctx', 'fsdp'))
- grad_gain_mlp: float32 [1024], P(('ctx', 'fsdp'))
All inputs are finite; a program needn't handle non-finite values.
Results may differ from a plain program's by a relative error of at most 0.015.
Values may be sent and summed in bfloat16 or wider, within the bound.
A program may use at most 256 MiB of HBM per device.

v0:
```python
import math
import jax
import jax.numpy as jnp
from jax import lax
from jax.sharding import PartitionSpec as P

HEAD_DIM = 64
EPSILON = 1e-05
ROPE_BASE = 160000.0


def normalize(tensor):
    centred = tensor - jnp.mean(tensor, axis=-1, keepdims=True)
    inv_std = lax.rsqrt(jnp.mean(centred * centred, axis=-1, keepdims=True) + EPSILON)
    return (centred * inv_std, inv_std)


def norm_back(grad_norm, normed, inv_std):
    return inv_std * (
        grad_norm
        - jnp.mean(grad_norm, axis=-1, keepdims=True)
        - normed * jnp.mean(grad_norm * normed, axis=-1, keepdims=True)
    )


def gelu_pair(tensor):
    cumul = 0.5 * (1.0 + jax.scipy.special.erf(tensor * 0.7071067811865476))
    density = jnp.exp(-0.5 * tensor * tensor) * 0.3989422804014327
    return (tensor * cumul, cumul + tensor * density)


def rope_tables(offset, length, head_size):
    positions = (offset + jnp.arange(length, dtype=jnp.int32)).astype(jnp.float32)
    inverse = ROPE_BASE ** (
        -jnp.arange(0, head_size, 2, dtype=jnp.int32).astype(jnp.float32) / head_size
    )
    angles = positions[:, None] * inverse[None, :]
    angles = jnp.concatenate([angles, angles], axis=-1)
    return (jnp.cos(angles)[:, None, :], jnp.sin(angles)[:, None, :])


def rotate(tensor, cos_table, sine_table):
    middle = tensor.shape[-1] // 2
    turned = jnp.concatenate([-tensor[..., middle:], tensor[..., :middle]], axis=-1)
    return tensor * cos_table + turned * sine_table


def rotate_back(gradient, cos_table, sine_table):
    middle = gradient.shape[-1] // 2
    scaled = gradient * sine_table
    turned = jnp.concatenate([scaled[..., middle:], -scaled[..., :middle]], axis=-1)
    return gradient * cos_table + turned


def rows_product(left, right):
    return lax.dot_general(
        left, right, (((1,), (1,)), ((), ())), preferred_element_type=jnp.float32
    )


def rows_contract(left, right):
    return lax.dot_general(
        left, right, (((0,), (0,)), ((), ())), preferred_element_type=jnp.float32
    )


def per_device(
    tokens, cotangent, gain_attn, gain_mlp, qkv_weight, out_weight, in_weight, down_weight
):
    f32 = jnp.float32
    bf16 = jnp.bfloat16
    qkv_full, out_full, in_full, down_full = (
        lax.all_gather(qkv_weight, "fsdp", axis=0, tiled=True),
        lax.all_gather(out_weight, "fsdp", axis=0, tiled=True),
        lax.all_gather(in_weight, "fsdp", axis=0, tiled=True),
        lax.all_gather(down_weight, "fsdp", axis=0, tiled=True),
    )
    tok_rows = tokens.shape[1]
    width = tokens.shape[2]
    hidden = down_full.shape[1]
    head_size = HEAD_DIM
    head_count = width // head_size
    scale = head_size ** (-0.5)
    offset = lax.axis_index("ctx") * tok_rows
    cos_table, sine_table = rope_tables(offset, tok_rows, head_size)
    resid = tokens[0].astype(f32)
    normed_a, inv_a = normalize(resid)
    act_a = (normed_a * gain_attn).astype(bf16)
    packed = rows_product(act_a, qkv_full)
    query_heads = rotate(
        packed[:, :width].reshape(tok_rows, head_count, head_size), cos_table, sine_table
    ).astype(bf16)
    key_heads = rotate(
        packed[:, width : 2 * width].reshape(tok_rows, head_count, head_size), cos_table, sine_table
    ).astype(bf16)
    value_send = packed[:, 2 * width :].astype(bf16)
    key_send = key_heads.reshape(tok_rows, width)
    value_heads = value_send.reshape(tok_rows, head_count, head_size)
    start_state = (
        jnp.zeros((tok_rows, head_count, head_size), f32),
        jnp.full((head_count, tok_rows), -1e30, f32),
        jnp.zeros((head_count, tok_rows), f32),
    )
    key_piece = lax.all_gather(key_send, "ctx", axis=0, tiled=True)
    value_piece = lax.all_gather(value_send, "ctx", axis=0, tiled=True)
    length = key_piece.shape[0]
    step_len = math.gcd(length, 1024)

    def attend_block(block_num, running):
        weighted, row_max, row_sum = running
        key_blk = lax.dynamic_slice_in_dim(key_piece, block_num * step_len, step_len, 0).reshape(
            step_len, head_count, head_size
        )
        value_blk = lax.dynamic_slice_in_dim(
            value_piece, block_num * step_len, step_len, 0
        ).reshape(step_len, head_count, head_size)
        scores = (
            jnp.einsum("qhd,khd->hqk", query_heads, key_blk, preferred_element_type=f32) * scale
        )
        new_max = jnp.maximum(row_max, jnp.max(scores, axis=-1))
        shrink = jnp.exp(row_max - new_max)
        weights = jnp.exp(scores - new_max[..., None])
        row_sum = row_sum * shrink + jnp.sum(weights, axis=-1)
        weighted = weighted * shrink.T[:, :, None] + jnp.einsum(
            "hqk,khd->qhd", weights.astype(bf16), value_blk, preferred_element_type=f32
        )
        return (weighted, new_max, row_sum)

    weighted, row_max, row_sum = lax.fori_loop(0, length // step_len, attend_block, start_state)
    log_sum = row_max + jnp.log(row_sum)
    mixed = (weighted / row_sum.T[:, :, None]).reshape(tok_rows, width).astype(bf16)
    middle = resid + rows_product(mixed, out_full)
    normed_m, inv_m = normalize(middle)
    act_m = (normed_m * gain_mlp).astype(bf16)
    inner = rows_product(act_m, in_full)
    gelu_val, gelu_slope = gelu_pair(inner[:, :hidden])
    gated = (gelu_val * inner[:, hidden:]).astype(bf16)
    output = middle + rows_product(gated, down_full)
    cot_rows = cotangent[0]
    grad_down = rows_contract(cot_rows, gated)
    grad_gated = jnp.dot(cot_rows, down_full, preferred_element_type=f32)
    grad_inner = jnp.concatenate(
        [grad_gated * inner[:, hidden:] * gelu_slope, grad_gated * gelu_val], axis=1
    ).astype(bf16)
    grad_in = rows_contract(grad_inner, act_m)
    grad_act_m = jnp.dot(grad_inner, in_full, preferred_element_type=f32)
    grad_gain_m = jnp.sum(grad_act_m * normed_m, axis=0)
    grad_middle = cot_rows.astype(f32) + norm_back(grad_act_m * gain_mlp, normed_m, inv_m)
    grad_mid_bf = grad_middle.astype(bf16)
    grad_out = rows_contract(grad_mid_bf, mixed)
    grad_mixed = jnp.dot(grad_mid_bf, out_full, preferred_element_type=f32).astype(bf16)
    grad_heads = grad_mixed.reshape(tok_rows, head_count, head_size)
    delta_rows = jnp.sum(
        grad_heads.astype(f32) * mixed.reshape(tok_rows, head_count, head_size).astype(f32), axis=-1
    )
    delta = delta_rows.T
    zeros_heads = jnp.zeros((tok_rows, head_count, head_size), f32)
    query_key_piece = lax.all_gather(key_send, "ctx", axis=0, tiled=True)
    query_value_piece = lax.all_gather(value_send, "ctx", axis=0, tiled=True)
    length = query_key_piece.shape[0]
    query_step_len = math.gcd(length, 1024)

    def query_grad_block(block_num, grad_query):
        key_blk = lax.dynamic_slice_in_dim(
            query_key_piece, block_num * query_step_len, query_step_len, 0
        ).reshape(query_step_len, head_count, head_size)
        value_blk = lax.dynamic_slice_in_dim(
            query_value_piece, block_num * query_step_len, query_step_len, 0
        ).reshape(query_step_len, head_count, head_size)
        scores = (
            jnp.einsum("qhd,khd->hqk", query_heads, key_blk, preferred_element_type=f32) * scale
        )
        probs = jnp.exp(scores - log_sum[..., None])
        grad_probs = jnp.einsum("qhd,khd->hqk", grad_heads, value_blk, preferred_element_type=f32)
        grad_scores = (probs * (grad_probs - delta[..., None])).astype(bf16)
        return (
            grad_query
            + jnp.einsum("hqk,khd->qhd", grad_scores, key_blk, preferred_element_type=f32) * scale
        )

    grad_query = lax.fori_loop(0, length // query_step_len, query_grad_block, zeros_heads)
    query_send = query_heads.reshape(tok_rows, width).astype(f32)
    grad_send = grad_mixed.astype(f32)
    query_piece = lax.all_gather(query_send, "ctx", axis=0, tiled=True)
    grad_piece = lax.all_gather(grad_send, "ctx", axis=0, tiled=True)
    log_piece = lax.all_gather(log_sum.T, "ctx", axis=0, tiled=True)
    delta_piece = lax.all_gather(delta_rows, "ctx", axis=0, tiled=True)
    length = query_piece.shape[0]
    key_step_len = math.gcd(length, 1024)

    def key_grad_block(block_num, running):
        grad_keys, grad_values = running
        query_blk = (
            lax.dynamic_slice_in_dim(query_piece, block_num * key_step_len, key_step_len, 0)
            .astype(bf16)
            .reshape(key_step_len, head_count, head_size)
        )
        grad_blk = (
            lax.dynamic_slice_in_dim(grad_piece, block_num * key_step_len, key_step_len, 0)
            .astype(bf16)
            .reshape(key_step_len, head_count, head_size)
        )
        log_blk = lax.dynamic_slice_in_dim(log_piece, block_num * key_step_len, key_step_len, 0).T
        delta_blk = lax.dynamic_slice_in_dim(
            delta_piece, block_num * key_step_len, key_step_len, 0
        ).T
        scores = (
            jnp.einsum("qhd,khd->hqk", query_blk, key_heads, preferred_element_type=f32) * scale
        )
        probs = jnp.exp(scores - log_blk[..., None])
        grad_values = grad_values + jnp.einsum(
            "hqk,qhd->khd", probs.astype(bf16), grad_blk, preferred_element_type=f32
        )
        grad_probs = jnp.einsum("qhd,khd->hqk", grad_blk, value_heads, preferred_element_type=f32)
        grad_scores = (probs * (grad_probs - delta_blk[..., None])).astype(bf16)
        grad_keys = (
            grad_keys
            + jnp.einsum("hqk,qhd->khd", grad_scores, query_blk, preferred_element_type=f32) * scale
        )
        return (grad_keys, grad_values)

    grad_keys, grad_values = lax.fori_loop(
        0, length // key_step_len, key_grad_block, (zeros_heads, zeros_heads)
    )
    grad_query = rotate_back(grad_query, cos_table, sine_table)
    grad_keys = rotate_back(grad_keys, cos_table, sine_table)
    grad_packed = jnp.concatenate(
        [
            grad_query.reshape(tok_rows, width),
            grad_keys.reshape(tok_rows, width),
            grad_values.reshape(tok_rows, width),
        ],
        axis=1,
    ).astype(bf16)
    grad_qkv = rows_contract(grad_packed, act_a)
    grad_act_a = jnp.dot(grad_packed, qkv_full, preferred_element_type=f32)
    grad_gain_a = jnp.sum(grad_act_a * normed_a, axis=0)
    grad_input = grad_middle + norm_back(grad_act_a * gain_attn, normed_a, inv_a)
    owned = (
        lax.psum_scatter(grad_qkv, ("ctx", "fsdp"), scatter_dimension=0, tiled=True),
        lax.psum_scatter(grad_out, ("ctx", "fsdp"), scatter_dimension=0, tiled=True),
        lax.psum_scatter(grad_in, ("ctx", "fsdp"), scatter_dimension=0, tiled=True),
        lax.psum_scatter(grad_down, ("ctx", "fsdp"), scatter_dimension=0, tiled=True),
        lax.psum_scatter(grad_gain_a, ("ctx", "fsdp"), scatter_dimension=0, tiled=True),
        lax.psum_scatter(grad_gain_m, ("ctx", "fsdp"), scatter_dimension=0, tiled=True),
    )
    return (
        output[None],
        grad_input[None],
        owned[0],
        owned[1],
        owned[2],
        owned[3],
        owned[4],
        owned[5],
    )


def solution(mesh):
    return jax.shard_map(
        per_device,
        mesh=mesh,
        in_specs=(
            P("fsdp", "ctx", None),
            P("fsdp", "ctx", None),
            P(),
            P(),
            P("fsdp", None),
            P("fsdp", None),
            P("fsdp", None),
            P("fsdp", None),
        ),
        out_specs=(
            P("fsdp", "ctx", None),
            P("fsdp", "ctx", None),
            P(("ctx", "fsdp"), None),
            P(("ctx", "fsdp"), None),
            P(("ctx", "fsdp"), None),
            P(("ctx", "fsdp"), None),
            P(("ctx", "fsdp")),
            P(("ctx", "fsdp")),
        ),
        check_vma=False,
    )
```

profile of v0, /device:TPU:14, one launch (start us, length us, event | category | flops | bytes accessed | tf_op | source)
XLA Modules:
  0.0 1275.8 jit_solution(7228493947482920155)
XLA Ops:
  9.6 80.5 %all-gather.9.cloned.1.call-done = bf16[3072,1024]{1,0:T(8,128)(2,1)} async-done(((bf16[1536,1024]{1,0:T(8,128)(2,1)}), bf16[3072,1024]{1,0:T(8,128)(2,1)}) %all-gather.9.cloned.1.call-update) | async-done | bytes 6291472 | tf_op jit(solution)/shard_map/all_gather | solution.py:73
  90.1 5.0 fusion.85
  106.7 47.2 %all-gather.11.cloned.1.call-done = bf16[2048,1024]{1,0:T(8,128)(2,1)} async-done(((bf16[128,1024]{1,0:T(8,128)(2,1)}), bf16[2048,1024]{1,0:T(8,128)(2,1)}) %all-gather.11.cloned.1.call-update) | async-done | bytes 4194320 | tf_op jit(solution)/shard_map/all_gather | solution.py:104
  153.9 6.5 copy.63
  160.4 44.6 %all-gather.13.cloned.1.call-done = bf16[2048,1024]{1,0:T(8,128)(2,1)} async-done(((bf16[128,1024]{1,0:T(8,128)(2,1)}), bf16[2048,1024]{1,0:T(8,128)(2,1)}) %all-gather.13.cloned.1.call-update) | async-done | bytes 4194320 | tf_op jit(solution)/shard_map/all_gather | solution.py:105
  205.0 6.5 copy.64
  211.5 29.9 %while.48 = (s32[]{:T(128)}, f32[128,16,64]{0,2,1:T(8,128)S(1)}, f32[16,128]{1,0:T(8,128)S(1)}, f32[16,128]{1,0:T(8,128)S(1)}, bf16[2048,1024]{0,1:T(8,128)(2,1)...) while((s32[]{:T(128)}, f32[128,16,64]{0,2,1:T(8,128)S(1)}, ...), condition=%wide.region_5.0_spmd.clone, body=%wide.region_2.0_spmd.clone.sunk | while | flops 554053632 | bytes 72745168 | solution.py:129
  214.6 4.8 bitcast_reduce_fusion.2
  219.4 5.3 fusion.148
  234.1 5.3 fusion.148
  244.3 127.5 %all-gather.17.cloned.1.call-done = bf16[5248,1024]{1,0:T(8,128)(2,1)} async-done(((bf16[2624,1024]{1,0:T(8,128)(2,1)}), bf16[5248,1024]{1,0:T(8,128)(2,1)}) %all-gather.17.cloned.1.call-update) | async-done | bytes 10747920 | tf_op jit(solution)/shard_map/all_gather | solution.py:75
  371.8 9.3 fusion.87
  381.1 62.2 %all-gather.19.cloned.1.call-done = bf16[1024,2624]{0,1:T(8,128)(2,1)} async-done(((bf16[512,2624]{0,1:T(8,128)(2,1)}), bf16[1024,2624]{0,1:T(8,128)(2,1)}) %all-gather.19.cloned.1.call-update) | async-done | bytes 5373968 | tf_op jit(solution)/shard_map/all_gather | solution.py:76
  443.3 5.3 fusion.48
  448.6 7.1 multiply_reduce_fusion
  460.0 7.7 convolution_bitcast_fusion
  467.7 12.1 copy.78
  483.0 15.4 %all_gather.39 = f32[2048,16]{0,1:T(8,128)S(1)} all-gather(f32[128,16]{0,1:T(8,128)S(1)} %bitcast.218), channel_id=1, replica_groups=mesh['ctx'=16,'fsdp'=2] {'ctx'}, dimensions={0}, use_global_device_ids=true | all-gather | bytes 139264 | tf_op jit(solution)/shard_map/all_gather | solution.py:186
  499.5 22.1 %all_gather.41 = f32[2048,16]{0,1:T(8,128)S(1)} all-gather(f32[128,16]{0,1:T(8,128)S(1)} %multiply_reduce_fusion.1), channel_id=1, replica_groups=mesh['ctx'=16,'fsdp'=2] {'ctx'}, dimensions={0}, use_global_device_ids=true | all-gather | bytes 139264 | tf_op jit(solution)/shard_map/all_gather | solution.py:187
  521.6 33.4 %while.49 = (s32[]{:T(128)}, f32[128,16,64]{0,2,1:T(8,128)}, bf16[2048,1024]{0,1:T(8,128)(2,1)}, bf16[128,16,64]{0,2,1:T(8,128)(2,1)S(1)}, f32[16,128]{1,0:T(8,1...) while((s32[]{:T(128)}, f32[128,16,64]{0,2,1:T(8,128)}, ...), condition=%wide.region_12.0_spmd.clone, body=%wide.region_11.0_spmd.clone.sunk | while | flops 816185344 | bytes 33079508 | solution.py:181
  530.2 8.1 fusion.157
  546.9 8.0 fusion.157
  555.0 65.2 %while.50 = (s32[]{:T(128)}, f32[128,16,64]{0,2,1:T(8,128)}, f32[128,16,64]{0,2,1:T(8,128)S(1)}, bf16[2048,1024]{1,0:T(8,128)(2,1)}, bf16[128,16,64]{0,2,1:T(8,1...) while((s32[]{:T(128)}, f32[128,16,64]{0,2,1:T(8,128)}, ...), condition=%wide.region_14.0_spmd.clone, body=%wide.region_13.0_spmd.clone.sunk | while | flops 1091174400 | bytes 53412036 | solution.py:222
  571.4 10.8 fusion.166
  582.2 5.5 fusion.167
  603.9 10.8 fusion.166
  614.7 5.5 fusion.167
  622.9 6.4 fusion.69
  630.8 9.2 fusion.50
  640.0 547.2 %fusion = f32[168,1024]{1,0:T(8,128)} fusion(f32[5248,1024]{1,0:T(8,128)} %fusion.50), kind=kCustom, calls=%all-reduce-scatter | all-reduce-scatter fusion | flops 5505025 | bytes 22183936
  1197.4 8.4 collective-permute-done
  1213.9 52.7 %all-reduce.4 = (f32[1024]{0:T(1024)S(1)}, f32[1024]{0:T(1024)S(1)}) all-reduce(f32[1024]{0:T(1024)S(1)} %get-tuple-element.613, f32[1024]{0:T(1024)S(1)} %copy-done.43), channel_id=6, replica_groups=mesh['ctx'=16,'fsdp'=2] {'ctx','fsdp'}, use_global_device_ids=true, to_apply=%region_22.0.clone | all-reduce | flops 2048 | bytes 16384
  (200 shorter events, 113.4 us)
Async XLA Ops:
  7.2 82.9 %copy-start.29 = (f32[1024]{0:T(1024)S(1)}, f32[1024]{0:T(1024)}, u32[]{:S(2)}) copy-start(f32[1024]{0:T(1024)} %param.16) | copy-start | bytes 12292
  7.2 82.9 %all-gather.9.cloned.1.call-start = ((), (), s32[]{:S(2)}) async-start(), calls=%async_computation.3 | async-start | bytes 9437184 | tf_op jit(solution)/shard_map/all_gather | solution.py:73
  7.9 146.0 %all-gather.11.cloned.1.call-start = ((), (), s32[]{:S(2)}) async-start(), calls=%async_computation.4 | async-start | bytes 4456448 | tf_op jit(solution)/shard_map/all_gather | solution.py:104
  8.2 89.4 %copy-start.25 = (f32[128,64]{0,1:T(8,128)}, f32[128,64]{0,1:T(8,128)S(1)}, u32[]{:S(2)}) copy-start(f32[128,64]{0,1:T(8,128)S(1)} %get-tuple-element.704) | copy-start | bytes 98308
  8.2 89.4 %copy-start.27 = (f32[128,64]{0,1:T(8,128)}, f32[128,64]{0,1:T(8,128)S(1)}, u32[]{:S(2)}) copy-start(f32[128,64]{0,1:T(8,128)S(1)} %get-tuple-element.703) | copy-start | bytes 98308
  9.3 85.8 %copy-start.35 = (f32[128]{0:T(128)}, f32[128]{0:T(128)S(1)}, u32[]{:S(2)}) copy-start(f32[128]{0:T(128)S(1)} %broadcast_multiply_fusion.8) | copy-start | bytes 1540
  9.6 85.5 %copy-start.37 = (f32[128]{0:T(128)}, f32[128]{0:T(128)S(1)}, u32[]{:S(2)}) copy-start(f32[128]{0:T(128)S(1)} %add_rsqrt_fusion.1) | copy-start | bytes 1540
  103.3 101.7 %all-gather.13.cloned.1.call-start = ((), (), s32[]{:S(2)}) async-start(), calls=%async_computation.5 | async-start | bytes 4456448 | tf_op jit(solution)/shard_map/all_gather | solution.py:105
  104.1 137.4 %all-gather.15.cloned.1.call-start = ((), (), s32[]{:S(2)}) async-start(), calls=%async_computation.6 | async-start | bytes 3145728 | tf_op jit(solution)/shard_map/all_gather | solution.py:74
  104.7 267.1 %all-gather.17.cloned.1.call-start = ((), (), s32[]{:S(2)}) async-start(), calls=%async_computation.7 | async-start | bytes 16121856 | tf_op jit(solution)/shard_map/all_gather | solution.py:75
  105.3 338.0 %all-gather.19.cloned.1.call-start = ((), (), s32[]{:S(2)}) async-start(), calls=%async_computation.8 | async-start | bytes 8060928 | tf_op jit(solution)/shard_map/all_gather | solution.py:76
  105.9 449.1 %all-gather.21.cloned.1.call-start = ((), (), s32[]{:S(2)}) async-start(), calls=%async_computation.9 | async-start | bytes 4456448 | tf_op jit(solution)/shard_map/all_gather | solution.py:184
  106.6 448.3 %all-gather.23.cloned.1.call-start = ((), (), s32[]{:S(2)}) async-start(), calls=%async_computation.10 | async-start | bytes 4456448 | tf_op jit(solution)/shard_map/all_gather | solution.py:185
  241.4 130.4 %copy-start.31 = (f32[1024]{0:T(1024)S(1)}, f32[1024]{0:T(1024)}, u32[]{:S(2)}) copy-start(f32[1024]{0:T(1024)} %param.17) | copy-start | bytes 12292
  244.0 211.6 %copy-start.1 = (f32[128,1024]{1,0:T(8,128)}, f32[128,1024]{1,0:T(8,128)S(1)}, u32[]{:S(2)}) copy-start(f32[128,1024]{1,0:T(8,128)S(1)} %get-tuple-element.706) | copy-start | bytes 1572868
  244.1 211.6 %copy-start.39 = (f32[128]{0:T(128)}, f32[128]{0:T(128)S(1)}, u32[]{:S(2)}) copy-start(f32[128]{0:T(128)S(1)} %broadcast_multiply_fusion.7) | copy-start | bytes 1540
  244.3 211.4 %copy-start.41 = (f32[128]{0:T(128)}, f32[128]{0:T(128)S(1)}, u32[]{:S(2)}) copy-start(f32[128]{0:T(128)S(1)} %add_rsqrt_fusion) | copy-start | bytes 1540
  244.3 199.0 %copy-start.20 = (bf16[1,128,1024]{2,1,0:T(8,128)(2,1)S(1)}, bf16[1,128,1024]{2,1,0:T(8,128)(2,1)}, u32[]{:S(2)}) copy-start(bf16[1,128,1024]{2,1,0:T(8,128)(2,1)} %param.15) | copy-start | bytes 786436
  448.5 7.1 copy-start.21
  448.6 7.1 copy-start.23
  448.6 7.4 copy-start.7
  457.1 811.7 %reduce-scatter.10.cloned.1.call-start = ((), (), s32[]{:S(2)}) async-start(), calls=%async_computation.12 | async-start | bytes 4325376 | tf_op jit(solution)/shard_map/reduce_scatter | solution.py:241
  460.0 808.9 %reduce-scatter.12.cloned.1.call-start = ((), (), s32[]{:S(2)}) async-start(), calls=%async_computation.13 | async-start | bytes 11354112
  479.8 789.0 %reduce-scatter.8.cloned.1.call-start = ((), (), s32[]{:S(2)}) async-start(), calls=%async_computation.11 | async-start | bytes 12976128 | tf_op jit(solution)/shard_map/reduce_scatter | solution.py:240
  521.6 33.4 %copy-start.6 = (bf16[128,16,64]{0,2,1:T(8,128)(2,1)S(1)}, bf16[128,16,64]{0,2,1:T(8,128)(2,1)}, u32[]{:S(2)}) copy-start(bf16[128,16,64]{0,2,1:T(8,128)(2,1)} %get-tuple-element.919) | copy-start | bytes 786436
  555.0 65.3 %copy-start.28 = (f32[128,64]{0,1:T(8,128)S(1)}, f32[128,64]{0,1:T(8,128)}, u32[]{:S(2)}) copy-start(f32[128,64]{0,1:T(8,128)} %copy-done.27) | copy-start | bytes 98308
  640.0 552.9 %copy-start.3 = (f32[128,5248]{1,0:T(8,128)S(1)}, f32[128,5248]{1,0:T(8,128)}, u32[]{:S(2)}) copy-start(f32[128,5248]{1,0:T(8,128)} %fusion.87) | copy-start | bytes 8060932
  1189.1 16.7 %collective-permute-start = (f32[124,1024]{1,0:T(8,128)}, f32[124,1024]{1,0:T(8,128)}, u32[]{:S(2)}, u32[]{:S(2)}) collective-permute-start(f32[124,1024]{1,0:T(8,128)} %slice.67), channel_id=1, source_target_pairs={{0,1},{1,2},{2,3},{3,4},{4,5},{5,6},{6,7},{7,8},{8,9},{9,10},{10,1... | collective-permute-start | bytes 1523720
  1197.4 12.5 copy-start.11
  1197.4 12.5 copy-start.13
  1197.4 12.5 copy-start.15
  1209.9 57.9 %copy-start.9 = (f32[128,1024]{1,0:T(8,128)S(1)}, f32[128,1024]{1,0:T(8,128)}, u32[]{:S(2)}) copy-start(f32[128,1024]{1,0:T(8,128)} %copy-done.8) | copy-start | bytes 1572868
  (26 other events, 55.5 us)
Sparse Core Ops, SparseCore 0:
  9.5 80.5 all-gather.8
  103.4 50.4 all-gather.10
  156.1 48.8 all-gather.12
  206.4 31.5 all-gather.14
  239.4 132.3 all-gather.16
  373.2 70.0 all-gather.18
  445.4 50.5 all-gather.20
  498.1 49.5 all-gather.22
  550.6 139.3 reduce-scatter.9
  696.4 204.9 reduce-scatter.11
  908.0 196.3 reduce-scatter.7
where the time goes:
time: 1280 us
  blocking collectives  637 us (50%)
  waiting for transfers between devices  373 us (29%)
  matrix products  152 us (12%)
  local copies, waits for them, and re-layouts  82 us (6%)
  between operations  15 us (1%)
    unnamed x2, blocking collectives  600 us
    all_gather x1, waiting for transfers between devices, per_device(): lax.all_gather(in_weight, 'fsdp', axis=0, tiled=True)  128 us
    all_gather x1, waiting for transfers between devices, per_device(): lax.all_gather(qkv_weight, 'fsdp', axis=0, tiled=True)  80.5 us
    all_gather x1, waiting for transfers between devices, per_device(): lax.all_gather(down_weight, 'fsdp', axis=0, tiled=True)  62.2 us
    all_gather x1, waiting for transfers between devices, per_device(): key_piece = lax.all_gather(key_send, 'ctx', axis=0, tiled=True)  47.2 us
    all_gather x1, waiting for transfers between devices, per_device(): value_piece = lax.all_gather(value_send, 'ctx', axis=0, tiled=True)  44.6 us
    unnamed x92, local copies, waits for them, and re-layouts  36 us
    dot_general x4, matrix products, rows_contract(): lax.dot_general(left, right, (((0,), (0,)), ((), ())), preferred_element_...  26 us
  transfers between devices with their start and end apart: 12, of which 6 were waited for; matrix products, arithmetic and copies ran while one was open for 61% of the time, Pallas kernels for 0%

commit v1 on v0

--- a/solution.py
+++ b/solution.py
@@ -7,6 +7,27 @@
 HEAD_DIM = 64
 EPSILON = 1e-05
 ROPE_BASE = 160000.0
+
+
+def laid_out(parts, dim):
+    shape = list(parts.shape[1:])
+    shape[dim] *= parts.shape[0]
+    return jnp.moveaxis(parts, 0, dim).reshape(shape)
+
+
+def grow_blocks(value, axis):
+    devices, index = (lax.axis_size(axis), lax.axis_index(axis))
+    tiles, bit = (value[None], 1)
+    while bit < devices:
+        other = lax.ppermute(tiles, axis, [(i, i ^ bit) for i in range(devices)])
+        low = index & bit == 0
+        tiles = jnp.concatenate([jnp.where(low, tiles, other), jnp.where(low, other, tiles)])
+        bit *= 2
+    return tiles
+
+
+def collect(shard, axis, dim):
+    return laid_out(grow_blocks(shard, axis), dim)
 
 
 def normalize(tensor):
@@ -70,7 +91,7 @@
     f32 = jnp.float32
     bf16 = jnp.bfloat16
     qkv_full, out_full, in_full, down_full = (
-        lax.all_gather(qkv_weight, "fsdp", axis=0, tiled=True),
+        collect(qkv_weight, "fsdp", 0),
         lax.all_gather(out_weight, "fsdp", axis=0, tiled=True),
         lax.all_gather(in_weight, "fsdp", axis=0, tiled=True),
         lax.all_gather(down_weight, "fsdp", axis=0, tiled=True),

time: 1280 us -> 1270 us (level)
  waiting for transfers between devices: 373 us -> 357 us
    all_gather x1 -> x0, waiting for transfers between devices: 80.5 us -> none  [per_device(): lax.all_gather(qkv_weight, 'fsdp', axis=0, tiled=True)]
    ppermute x0 -> x1, waiting for transfers between devices: none -> 64.2 us  [grow_blocks(): other = lax.ppermute(tiles, axis, [(i, i ^ bit) for i in range(devices)])]
    unnamed x92 -> x94, local copies, waits for them, and re-layouts: 36 us -> 36.4 us
  transfers between devices with their start and end apart: 12 -> 12, of which waited for: 6 -> 6; matrix products, arithmetic and copies ran while one was open for 61% -> 62% of each run, Pallas kernels for 0% -> 0%
where the time goes in v1:
time: 1270 us; the launch traced here: 1260 us
  blocking collectives  637 us (50%)
  waiting for transfers between devices  357 us (28%)
  matrix products  149 us (12%)
  local copies, waits for them, and re-layouts  84.2 us (7%)
  other arithmetic  15.8 us (1%)
  between operations  15.3 us (1%)
    unnamed x2, blocking collectives  600 us
    all_gather x1, waiting for transfers between devices, per_device(): lax.all_gather(in_weight, 'fsdp', axis=0, tiled=True)  128 us
    ppermute x1, waiting for transfers between devices, grow_blocks(): other = lax.ppermute(tiles, axis, [(i, i ^ bit) for i in range(devices)])  64.2 us
    all_gather x1, waiting for transfers between devices, per_device(): lax.all_gather(down_weight, 'fsdp', axis=0, tiled=True)  62.2 us
    all_gather x1, waiting for transfers between devices, per_device(): key_piece = lax.all_gather(key_send, 'ctx', axis=0, tiled=True)  47.4 us
    all_gather x1, waiting for transfers between devices, per_device(): value_piece = lax.all_gather(value_send, 'ctx', axis=0, tiled=True)  44.6 us
    unnamed x94, local copies, waits for them, and re-layouts  36.4 us
    dot_general x4, matrix products, rows_contract(): lax.dot_general(left, right, (((0,), (0,)), ((), ())), preferred_element_...  26 us
  transfers between devices with their start and end apart: 12, of which 6 were waited for; matrix products, arithmetic and copies ran while one was open for 62% of the time, Pallas kernels for 0%

profile of v1, /device:TPU:14, one launch (start us, length us, event | category | flops | bytes accessed | tf_op | source)
XLA Modules:
  0.0 1263.8 jit_solution(2152691232269389803)
XLA Ops:
  13.1 64.2 %collective-permute-done = bf16[1,1536,1024]{2,1,0:T(8,128)(2,1)S(1)} collective-permute-done((bf16[1,1536,1024]{2,1,0:T(8,128)(2,1)}, bf16[1,1536,1024]{2,1,0:T(8,128)(2,1)S(1)}, u32[]{:S(2)}, u32[]{:S(2)}) %collective-permute-start) | collective-permute-done | bytes 3145760 | tf_op jit(solution)/shard_map/ppermute | solution.py:22
  94.4 47.4 %all-gather.8.cloned.1.call-done = bf16[2048,1024]{1,0:T(8,128)(2,1)} async-done(((bf16[128,1024]{1,0:T(8,128)(2,1)}), bf16[2048,1024]{1,0:T(8,128)(2,1)}) %all-gather.8.cloned.1.call-update) | async-done | bytes 4194320 | tf_op jit(solution)/shard_map/all_gather | solution.py:125
  141.8 6.5 copy.63
  148.3 44.6 %all-gather.10.cloned.1.call-done = bf16[2048,1024]{1,0:T(8,128)(2,1)} async-done(((bf16[128,1024]{1,0:T(8,128)(2,1)}), bf16[2048,1024]{1,0:T(8,128)(2,1)}) %all-gather.10.cloned.1.call-update) | async-done | bytes 4194320 | tf_op jit(solution)/shard_map/all_gather | solution.py:126
  192.9 6.5 copy.64
  199.4 29.9 %while.48 = (s32[]{:T(128)}, f32[128,16,64]{0,2,1:T(8,128)S(1)}, f32[16,128]{1,0:T(8,128)S(1)}, f32[16,128]{1,0:T(8,128)S(1)}, bf16[2048,1024]{0,1:T(8,128)(2,1)...) while((s32[]{:T(128)}, f32[128,16,64]{0,2,1:T(8,128)S(1)}, ...), condition=%wide.region_5.6_spmd.clone, body=%wide.region_2.5_spmd.clone.sunk | while | flops 554053632 | bytes 72745168 | solution.py:150
  202.5 4.8 bitcast_reduce_fusion.2
  207.3 5.3 fusion.158
  217.2 4.8 bitcast_reduce_fusion.2
  222.0 5.3 fusion.158
  232.2 127.7 %all-gather.14.cloned.1.call-done = bf16[5248,1024]{1,0:T(8,128)(2,1)} async-done(((bf16[2624,1024]{1,0:T(8,128)(2,1)}), bf16[5248,1024]{1,0:T(8,128)(2,1)}) %all-gather.14.cloned.1.call-update) | async-done | bytes 10747920 | tf_op jit(solution)/shard_map/all_gather | solution.py:96
  359.9 9.3 fusion.97
  369.1 62.2 %all-gather.16.cloned.1.call-done = bf16[1024,2624]{0,1:T(8,128)(2,1)} async-done(((bf16[512,2624]{0,1:T(8,128)(2,1)}), bf16[1024,2624]{0,1:T(8,128)(2,1)}) %all-gather.16.cloned.1.call-update) | async-done | bytes 5373968 | tf_op jit(solution)/shard_map/all_gather | solution.py:97
  431.3 5.3 fusion.48
  436.6 7.1 multiply_reduce_fusion
  448.1 7.7 convolution_bitcast_fusion
  455.7 12.1 copy.78
  471.1 15.4 %all_gather.35 = f32[2048,16]{0,1:T(8,128)S(1)} all-gather(f32[128,16]{0,1:T(8,128)S(1)} %bitcast.227), channel_id=1, replica_groups=mesh['ctx'=16,'fsdp'=2] {'ctx'}, dimensions={0}, use_global_device_ids=true | all-gather | bytes 139264 | tf_op jit(solution)/shard_map/all_gather | solution.py:207
  487.5 22.2 %all_gather.37 = f32[2048,16]{0,1:T(8,128)S(1)} all-gather(f32[128,16]{0,1:T(8,128)S(1)} %multiply_reduce_fusion.1), channel_id=1, replica_groups=mesh['ctx'=16,'fsdp'=2] {'ctx'}, dimensions={0}, use_global_device_ids=true | all-gather | bytes 139264 | tf_op jit(solution)/shard_map/all_gather | solution.py:208
  509.7 33.4 %while.49 = (s32[]{:T(128)}, f32[128,16,64]{0,2,1:T(8,128)}, bf16[2048,1024]{0,1:T(8,128)(2,1)}, bf16[128,16,64]{0,2,1:T(8,128)(2,1)S(1)}, f32[16,128]{1,0:T(8,1...) while((s32[]{:T(128)}, f32[128,16,64]{0,2,1:T(8,128)}, ...), condition=%wide.region_12.13_spmd.clone, body=%wide.region_11.12_spmd.clone.sunk | while | flops 816185344 | bytes 33079508 | solution.py:202
  518.4 8.1 fusion.167
  535.1 8.0 fusion.167
  543.1 65.2 %while.50 = (s32[]{:T(128)}, f32[128,16,64]{0,2,1:T(8,128)}, f32[128,16,64]{0,2,1:T(8,128)S(1)}, bf16[2048,1024]{1,0:T(8,128)(2,1)}, bf16[128,16,64]{0,2,1:T(8,1...) while((s32[]{:T(128)}, f32[128,16,64]{0,2,1:T(8,128)}, ...), condition=%wide.region_14.15_spmd.clone, body=%wide.region_13.14_spmd.clone.sunk | while | flops 1091174400 | bytes 53412036 | solution.py:243
  559.5 10.8 fusion.176
  570.3 5.5 fusion.177
  592.0 10.8 fusion.176
  602.8 5.5 fusion.177
  611.0 6.4 fusion.72
  618.9 9.2 fusion.50
  628.1 546.9 %fusion = f32[168,1024]{1,0:T(8,128)} fusion(f32[5248,1024]{1,0:T(8,128)} %fusion.50), kind=kCustom, calls=%all-reduce-scatter | all-reduce-scatter fusion | flops 5505025 | bytes 22183936
  1185.2 8.1 collective-permute-done.1
  1201.4 52.8 %all-reduce.4 = (f32[1024]{0:T(1024)S(1)}, f32[1024]{0:T(1024)S(1)}) all-reduce(f32[1024]{0:T(1024)S(1)} %get-tuple-element.613, f32[1024]{0:T(1024)S(1)} %copy-done.44), channel_id=6, replica_groups=mesh['ctx'=16,'fsdp'=2] {'ctx','fsdp'}, use_global_device_ids=true, to_apply=%region_22.23.clone | all-reduce | flops 2048 | bytes 16384
  (203 shorter events, 117.6 us)
Async XLA Ops:
  7.2 134.6 %all-gather.8.cloned.1.call-start = ((), (), s32[]{:S(2)}) async-start(), calls=%async_computation.3 | async-start | bytes 4456448 | tf_op jit(solution)/shard_map/all_gather | solution.py:125
  7.2 70.1 %collective-permute-start = (bf16[1,1536,1024]{2,1,0:T(8,128)(2,1)}, bf16[1,1536,1024]{2,1,0:T(8,128)(2,1)S(1)}, u32[]{:S(2)}, u32[]{:S(2)}) collective-permute-start(bf16[1,1536,1024]{2,1,0:T(8,128)(2,1)} %bitcast.211), channel_id=1, source_target_pairs={{0,1},{1,0},{2,3},{3,2},{4,5},{5,4},{6,7},{7,6},{8,9},{9,8},{10,11... | collective-permute-start | bytes 9437192 | tf_op jit(solution)/shard_map/ppermute | solution.py:22
  8.0 77.4 %copy-start.26 = (f32[128,64]{0,1:T(8,128)}, f32[128,64]{0,1:T(8,128)S(1)}, u32[]{:S(2)}) copy-start(f32[128,64]{0,1:T(8,128)S(1)} %get-tuple-element.706) | copy-start | bytes 98308
  8.0 77.4 %copy-start.28 = (f32[128,64]{0,1:T(8,128)}, f32[128,64]{0,1:T(8,128)S(1)}, u32[]{:S(2)}) copy-start(f32[128,64]{0,1:T(8,128)S(1)} %get-tuple-element.705) | copy-start | bytes 98308
  11.9 68.3 %copy-start.36 = (f32[128]{0:T(128)}, f32[128]{0:T(128)S(1)}, u32[]{:S(2)}) copy-start(f32[128]{0:T(128)S(1)} %broadcast_multiply_fusion.8) | copy-start | bytes 1540
  13.1 67.1 %copy-start.38 = (f32[128]{0:T(128)}, f32[128]{0:T(128)S(1)}, u32[]{:S(2)}) copy-start(f32[128]{0:T(128)S(1)} %add_rsqrt_fusion.1) | copy-start | bytes 1540
  91.1 101.8 %all-gather.10.cloned.1.call-start = ((), (), s32[]{:S(2)}) async-start(), calls=%async_computation.4 | async-start | bytes 4456448 | tf_op jit(solution)/shard_map/all_gather | solution.py:126
  91.9 137.5 %all-gather.12.cloned.1.call-start = ((), (), s32[]{:S(2)}) async-start(), calls=%async_computation.5 | async-start | bytes 3145728 | tf_op jit(solution)/shard_map/all_gather | solution.py:95
  92.6 267.3 %all-gather.14.cloned.1.call-start = ((), (), s32[]{:S(2)}) async-start(), calls=%async_computation.6 | async-start | bytes 16121856 | tf_op jit(solution)/shard_map/all_gather | solution.py:96
  93.2 338.1 %all-gather.16.cloned.1.call-start = ((), (), s32[]{:S(2)}) async-start(), calls=%async_computation.7 | async-start | bytes 8060928 | tf_op jit(solution)/shard_map/all_gather | solution.py:97
  93.8 449.3 %all-gather.18.cloned.1.call-start = ((), (), s32[]{:S(2)}) async-start(), calls=%async_computation.8 | async-start | bytes 4456448 | tf_op jit(solution)/shard_map/all_gather | solution.py:205
  94.3 448.7 %all-gather.20.cloned.1.call-start = ((), (), s32[]{:S(2)}) async-start(), calls=%async_computation.9 | async-start | bytes 4456448 | tf_op jit(solution)/shard_map/all_gather | solution.py:206
  207.3 5.8 copy-start
  229.3 130.6 %copy-start.32 = (f32[1024]{0:T(1024)S(1)}, f32[1024]{0:T(1024)}, u32[]{:S(2)}) copy-start(f32[1024]{0:T(1024)} %param.17) | copy-start | bytes 12292
  231.9 211.8 %copy-start.2 = (f32[128,1024]{1,0:T(8,128)}, f32[128,1024]{1,0:T(8,128)S(1)}, u32[]{:S(2)}) copy-start(f32[128,1024]{1,0:T(8,128)S(1)} %get-tuple-element.708) | copy-start | bytes 1572868
  231.9 211.8 %copy-start.40 = (f32[128]{0:T(128)}, f32[128]{0:T(128)S(1)}, u32[]{:S(2)}) copy-start(f32[128]{0:T(128)S(1)} %broadcast_multiply_fusion.7) | copy-start | bytes 1540
  232.2 211.6 %copy-start.42 = (f32[128]{0:T(128)}, f32[128]{0:T(128)S(1)}, u32[]{:S(2)}) copy-start(f32[128]{0:T(128)S(1)} %add_rsqrt_fusion) | copy-start | bytes 1540
  232.2 199.1 %copy-start.21 = (bf16[1,128,1024]{2,1,0:T(8,128)(2,1)S(1)}, bf16[1,128,1024]{2,1,0:T(8,128)(2,1)}, u32[]{:S(2)}) copy-start(bf16[1,128,1024]{2,1,0:T(8,128)(2,1)} %param.15) | copy-start | bytes 786436
  436.6 7.1 copy-start.22
  436.6 7.1 copy-start.24
  436.6 7.4 copy-start.8
  445.2 811.3 %reduce-scatter.10.cloned.1.call-start = ((), (), s32[]{:S(2)}) async-start(), calls=%async_computation.11 | async-start | bytes 4325376 | tf_op jit(solution)/shard_map/reduce_scatter | solution.py:262
  448.0 808.5 %reduce-scatter.12.cloned.1.call-start = ((), (), s32[]{:S(2)}) async-start(), calls=%async_computation.12 | async-start | bytes 11354112
  467.9 788.7 %reduce-scatter.8.cloned.1.call-start = ((), (), s32[]{:S(2)}) async-start(), calls=%async_computation.10 | async-start | bytes 12976128 | tf_op jit(solution)/shard_map/reduce_scatter | solution.py:261
  509.7 33.4 %copy-start.7 = (bf16[128,16,64]{0,2,1:T(8,128)(2,1)S(1)}, bf16[128,16,64]{0,2,1:T(8,128)(2,1)}, u32[]{:S(2)}) copy-start(bf16[128,16,64]{0,2,1:T(8,128)(2,1)} %get-tuple-element.921) | copy-start | bytes 786436
  543.1 65.3 %copy-start.29 = (f32[128,64]{0,1:T(8,128)S(1)}, f32[128,64]{0,1:T(8,128)}, u32[]{:S(2)}) copy-start(f32[128,64]{0,1:T(8,128)} %copy-done.28) | copy-start | bytes 98308
  628.1 552.6 %copy-start.4 = (f32[128,5248]{1,0:T(8,128)S(1)}, f32[128,5248]{1,0:T(8,128)}, u32[]{:S(2)}) copy-start(f32[128,5248]{1,0:T(8,128)} %fusion.97) | copy-start | bytes 8060932
  1176.9 16.4 %collective-permute-start.1 = (f32[124,1024]{1,0:T(8,128)}, f32[124,1024]{1,0:T(8,128)}, u32[]{:S(2)}, u32[]{:S(2)}) collective-permute-start(f32[124,1024]{1,0:T(8,128)} %slice.67), channel_id=1, source_target_pairs={{0,1},{1,2},{2,3},{3,4},{4,5},{5,6},{6,7},{7,8},{8,9},{9,10},{10,1... | collective-permute-start | bytes 1523720
  1185.2 12.2 copy-start.12
  1185.2 12.2 copy-start.14
  1185.2 12.2 copy-start.16
  1197.4 58.0 %copy-start.10 = (f32[128,1024]{1,0:T(8,128)S(1)}, f32[128,1024]{1,0:T(8,128)}, u32[]{:S(2)}) copy-start(f32[128,1024]{1,0:T(8,128)} %copy-done.9) | copy-start | bytes 1572868
  (27 other events, 52.2 us)
Sparse Core Ops, SparseCore 0:
  91.2 50.5 all-gather.7
  144.0 48.8 all-gather.9
  194.5 31.5 all-gather.11
  227.5 132.3 all-gather.13
  361.3 70.0 all-gather.15
  433.3 50.4 all-gather.17
  486.0 49.4 all-gather.19
  538.4 139.8 reduce-scatter.9
  684.9 205.1 reduce-scatter.11
  896.5 194.0 reduce-scatter.7
